TPU v7x, 32 devices: a whole 2x2x4 slice. The times are simulated.
32 devices in a mesh: groups: 2 (over y), expert: 8 (over z, x), sub: 2 (over core).
Axes of the slice: x: 2, y: 2, z: 4, core: 2. Of those that a mesh axis runs over, the one named last changes fastest.
Arguments:
- stream_in: bfloat16 [1024, 3072], P(('groups', 'expert'), 'sub'), parts along dimension 0, may hold values from -0.29882812 to 0.29882812
- queries: bfloat16 [1024, 3072], P(('groups', 'expert'), 'sub'), parts along dimension 0, may hold values from -6 to 6
- kv_new: bfloat16 [2, 1024, 1024], P(None, ('groups', 'expert'), 'sub'), parts along dimension 1, may hold values from -6 to 6
- paged_key_value_cache: bfloat16 [2, 32, 4, 1024], P(None, ('groups', 'expert'), None, 'sub'), parts along dimension 1, may hold values from -6 to 6
- page_table: int32 [16, 8], P(('groups', 'expert')), parts along dimension 0, may hold values from 0 to 15, as said below
- prefix_len: int32 [16], P(('groups', 'expert')), parts along dimension 0, may hold values from 8 to 32
- norm_gain: float32 [3072], replicated, may hold values from 0.5 to 1.5
- w_router: bfloat16 [3072, 8], replicated, may hold values from -0.21875 to 0.21875
- expert_ids: int32 [1024, 2], P(('groups', 'expert')), parts along dimension 0, may hold values from 0 to 7, as said below
- w_in: bfloat16 [2, 3072, 65536], P(None, None, ('expert', 'sub')), may hold values from -0.109375 to 0.109375
Outputs:
- stream: bfloat16 [1024, 3072], P(('groups', 'expert'), 'sub'), parts along dimension 0
- expert_hidden: bfloat16 [272, 65536], P('groups', ('expert', 'sub')), parts along dimension 0
There are 2 independent parts, one for each index of `groups`. A program takes and returns all parts, laid end to end along the dimension named above; an argument that names none is the same for every part. Nothing has to cross between parts.
Inputs may be any that keep to these rules, and one draw needn't show every extreme that they name: `expert_ids`: each row names two different experts. The rows of one request name each expert at most 17 times, and one expert is named exactly 17 times by the rows of every request. `page_table`: the pages of one row lie in different shards: page // 2 differs along a row. Requests share leading pages.
All inputs are finite; a program needn't handle non-finite values.
Results may differ from a plain program's by a relative error of at most 0.018.
Values may be sent and summed in bfloat16 or wider, within the bound.
No kernel may reach another device: no remote copies, remote signals or barrier semaphores. Data moves between devices by JAX's collectives and lax.ppermute only.
A program may use at most 128 MiB of HBM per device.

v0:
```python
import math

import jax
import jax.numpy as jnp
from jax import lax
from jax.sharding import PartitionSpec as P

HEAD_WIDTH = 128
EXPERTS = 8
TOP = 2
CAP = 17


def for_sending(array):

    def short(part):
        return part.astype(jnp.bfloat16) if part.dtype == jnp.float32 else part

    return jax.tree.map(short, array)


def partner(array, axis, apart):
    return lax.ppermute(array, axis, [(i, i ^ 1 << apart) for i in range(lax.axis_size(axis))])


def from_behind(value, axis, steps):
    count = lax.axis_size(axis)
    pairs = [(source, (source + steps) % count) for source in range(count)]
    return lax.ppermute(value, axis, pairs)


def attend(query_rows, key_rows, prefix_length, head_size):
    tokens_here = query_rows.shape[0]
    length = key_rows.shape[1]
    kv_heads = key_rows.shape[2] // head_size
    grouped = query_rows.shape[1] // head_size // kv_heads
    query_f = query_rows.reshape(tokens_here, kv_heads, grouped, head_size).astype(jnp.float32)
    keys_f = key_rows[0].reshape(length, kv_heads, head_size).astype(jnp.float32)
    values_f = key_rows[1].reshape(length, kv_heads, head_size).astype(jnp.float32)
    scores = jnp.einsum("tkgd,lkd->kgtl", query_f, keys_f) * (1.0 / math.sqrt(head_size))
    prefix_span = length - tokens_here
    places = jnp.arange(length)[None, :]
    rows_at = jnp.arange(tokens_here)[:, None]
    is_live = jnp.where(
        places < prefix_span, places < prefix_length, places - prefix_span <= rows_at
    )
    scores = jnp.where(is_live, scores, -1e30)
    largest = jnp.max(scores, axis=-1, keepdims=True)
    exponent = jnp.exp(scores - largest)
    weights = (exponent / jnp.sum(exponent, axis=-1, keepdims=True)).astype(jnp.bfloat16)
    mixed_heads = jnp.einsum("kgtl,lkd->tkgd", weights.astype(jnp.float32), values_f)
    return mixed_heads.reshape(tokens_here, -1).astype(jnp.bfloat16)


def pick_block(stack_rows, position):
    return lax.dynamic_index_in_dim(stack_rows, position, 0, keepdims=False)


def spread(kept_rows, kept_shares, own_index, level_values):
    for depth_bit in range(level_values):
        partner_rows, partner_shares = (
            partner(for_sending(kept_rows), "expert", depth_bit).astype(kept_rows.dtype),
            partner(for_sending(kept_shares), "expert", depth_bit).astype(kept_shares.dtype),
        )
        high_bit = (own_index >> depth_bit) % 2 == 1
        lower_rows = jnp.where(high_bit, partner_rows, kept_rows)
        upper_rows = jnp.where(high_bit, kept_rows, partner_rows)
        lower_shares = jnp.where(high_bit, partner_shares, kept_shares)
        upper_shares = jnp.where(high_bit, kept_shares, partner_shares)
        kept_rows = jnp.concatenate([lower_rows, upper_rows], axis=0)
        kept_shares = jnp.concatenate([lower_shares, upper_shares], axis=0)
    return (kept_rows, kept_shares)


def shards(
    stream_in,
    queries,
    kv_new,
    paged_key_value_cache,
    page_table,
    prefix_len,
    norm_gain,
    w_router,
    expert_ids,
    w_in,
):
    expert_count = lax.axis_size("expert")
    group_width = expert_count // EXPERTS
    level_values = group_width.bit_length() - 1
    own_index = lax.axis_index("expert")
    own_group = own_index // group_width
    shard_pages = paged_key_value_cache.shape[1]
    page_list = page_table[0]
    owners = page_list // shard_pages
    inside = page_list % shard_pages
    owner_hot = owners[None, :] == jnp.arange(expert_count, dtype=jnp.int32)[:, None]
    wanted = jnp.sum(jnp.where(owner_hot, inside[None, :], 0), axis=1)
    asked_for = lax.all_to_all(wanted[:, None], "expert", split_axis=0, concat_axis=0, tiled=True)
    served = jnp.take(paged_key_value_cache, asked_for[:, 0], axis=1)
    arrived = lax.all_to_all(served, "expert", split_axis=1, concat_axis=1, tiled=True)
    prefix_pages = jnp.take(arrived, owners, axis=1)
    prefix_row_block = prefix_pages.reshape(2, -1, prefix_pages.shape[-1])
    key_rows = jnp.concatenate([prefix_row_block, kv_new], axis=1)
    attended = attend(queries, key_rows, prefix_len[0], HEAD_WIDTH)
    stream_part = (stream_in.astype(jnp.float32) + attended.astype(jnp.float32)).astype(
        jnp.bfloat16
    )
    stream = lax.all_gather(stream_part, "sub", axis=1, tiled=True)
    stream_f = stream.astype(jnp.float32)
    scale_rows = lax.rsqrt(jnp.mean(stream_f * stream_f, axis=-1, keepdims=True) + 1e-05)
    normed = (stream_f * scale_rows * norm_gain).astype(jnp.bfloat16)
    logits = jnp.dot(normed, w_router, preferred_element_type=jnp.float32)
    chosen = jnp.take_along_axis(logits, expert_ids, axis=1)
    gate_share = jax.nn.sigmoid(chosen - chosen[:, ::-1])
    row_count = stream_in.shape[0]
    routes = expert_ids.reshape(-1)
    route_count = routes.shape[0]
    expert_hot = (routes[:, None] == jnp.arange(EXPERTS, dtype=jnp.int32)[None, :]).astype(
        jnp.int32
    )
    route_rank = jnp.sum((jnp.cumsum(expert_hot, axis=0) - 1) * expert_hot, axis=1)
    slot_hot = (route_rank[:, None] == jnp.arange(CAP, dtype=jnp.int32)[None, :]).astype(
        jnp.float32
    )
    row_hot = ((jnp.arange(route_count) // TOP)[:, None] == jnp.arange(row_count)[None, :]).astype(
        jnp.float32
    )
    route_place = expert_hot.astype(jnp.float32)[:, :, None] * slot_hot[:, None, :]
    picker = jnp.einsum("rem,rt->emt", route_place, row_hot)
    shares = jnp.einsum("rem,r->em", route_place, gate_share.reshape(-1))
    outgoing = jnp.einsum(
        "emt,td->emd", picker.astype(jnp.bfloat16), normed, preferred_element_type=jnp.float32
    ).astype(jnp.bfloat16)
    arrived_rows = [pick_block(outgoing, own_group)]
    arrived_shares = [pick_block(shares, own_group)]
    for stride in range(1, EXPERTS):
        target = (own_group + stride) % EXPERTS
        rows_in, shares_in = (
            from_behind(pick_block(outgoing, target), "expert", stride * group_width),
            from_behind(
                pick_block(shares, target).astype(jnp.bfloat16), "expert", stride * group_width
            ).astype(jnp.float32),
        )
        arrived_rows.append(rows_in)
        arrived_shares.append(shares_in)
    home_order = (own_group - jnp.arange(EXPERTS, dtype=jnp.int32)) % EXPERTS
    rows_by_source = jnp.take(jnp.stack(arrived_rows), home_order, axis=0)
    shares_by_source = jnp.take(jnp.stack(arrived_shares), home_order, axis=0)
    kept_rows, kept_shares = spread(
        rows_by_source[None], shares_by_source[None], own_index, level_values
    )
    slot_rows = kept_rows.reshape(-1, kept_rows.shape[-1])
    slot_shares = kept_shares.reshape(-1)
    gate_part = jnp.dot(slot_rows, w_in[0], preferred_element_type=jnp.float32)
    up_part = jnp.dot(slot_rows, w_in[1], preferred_element_type=jnp.float32)
    hidden = (jax.nn.silu(gate_part) * up_part * slot_shares[:, None]).astype(jnp.bfloat16)
    return (stream_part, hidden)


def solution(mesh):
    placed = (
        P(("groups", "expert"), "sub"),
        P(("groups", "expert"), "sub"),
        P(None, ("groups", "expert"), "sub"),
        P(None, ("groups", "expert"), None, "sub"),
        P(("groups", "expert"), None),
        P(("groups", "expert")),
        P(),
        P(),
        P(("groups", "expert"), None),
        P(None, None, ("expert", "sub")),
    )
    return jax.shard_map(
        shards,
        mesh=mesh,
        in_specs=placed,
        out_specs=(P(("groups", "expert"), "sub"), P("groups", ("expert", "sub"))),
        check_vma=False,
    )
```

profile of v0, /device:TPU:0, one launch (start us, length us, event | category | flops | bytes accessed | tf_op | source)
XLA Modules:
  0.0 103.6 jit_solution(13297511967904677882)
XLA Ops:
  0.7 0.7 fusion.77
  1.5 0.7 copy.83
  2.2 7.3 %all-to-all-start = ((s32[8,1,1]{2,1,0:T(1,128)}), s32[8,1,1]{2,1,0:T(1,128)S(1)}, u32[]{:S(2)}, u32[]{:S(2)}) async-start(s32[8,1,1]{2,1,0:T(1,128)} %copy.83), calls=%async_computation | async-start | bytes 8192 | tf_op jit(solution)/shard_map/all_to_all | solution.py:98
  9.5 0.7 fusion.60
  10.2 0.7 bitcast_or_fusion
  10.9 0.8 copy.90
  12.9 3.0 %all-to-all-done = s32[8,1,1]{2,1,0:T(1,128)S(1)} async-done(((s32[8,1,1]{2,1,0:T(1,128)}), s32[8,1,1]{2,1,0:T(1,128)S(1)}, u32[]{:S(2)}, u32[]{:S(2)}) %all-to-all-start) | async-done | bytes 64 | tf_op jit(solution)/shard_map/all_to_all | solution.py:98
  16.1 0.7 compare_and_fusion.1
  16.8 1.3 %gather_fusion = bf16[8,2,4,512]{3,2,1,0:T(4,128)(2,1)S(1)} fusion(bf16[2,2,4,512]{3,2,1,0:T(4,128)(2,1)} %param.13, s32[1024]{0:T(1024)S(1)} %pad_clamp_fusion.2), kind=kCustom, calls=%fused_computation | custom fusion | bytes 131104 | tf_op jit(solution)/shard_map/jit(_take)/gather | solution.py:99
  18.1 0.7 select_bitcast_fusion
  18.9 3.4 %all-to-all-start.1 = ((bf16[2,8,4,512]{3,2,0,1:T(4,128)(2,1)}), bf16[2,8,4,512]{3,2,0,1:T(4,128)(2,1)S(1)}, u32[]{:S(2)}, u32[]{:S(2)}) async-start(bf16[2,8,4,512]{3,2,0,1:T(4,128)(2,1)} %select_bitcast_fusion), calls=%async_computation.1 | async-start | bytes 131072 | tf_op jit(solution)/shard_map/all_to_all | solution.py:100
  22.9 6.1 %all-to-all-done.1 = bf16[2,8,4,512]{3,2,0,1:T(4,128)(2,1)S(1)} async-done(((bf16[2,8,4,512]{3,2,0,1:T(4,128)(2,1)}), bf16[2,8,4,512]{3,2,0,1:T(4,128)(2,1)S(1)}, u32[]{:S(2)}, u32[]{:S(2)}) %all-to-all-start.1) | async-done | bytes 65568 | tf_op jit(solution)/shard_map/all_to_all | solution.py:100
  30.7 1.4 %fusion.21 = f32[64,4,3,128]{3,0,2,1:T(8,128)S(1)} fusion(f32[4,3,64]{2,1,0:T(4,128)S(1)} %fusion.81, bf16[96,4,128,1]{2,1,0,3:T(4,128)(2,1)S(1)} %bitcast.148, f32[4,3,64,96]{3,2,1,0:T(8,128)S(1)} %fusion.19), kind=kOutput, calls=%fused_computation.24 | convolution fusion | flops 19293024 | bytes 789504 | tf_op jit(solution)/shard_map/kgtl,lkd->tkgd/dot_general | solution.py:51
  33.1 2.1 %all_gather.3 = bf16[64,3072]{1,0:T(8,128)(2,1)S(1)} all-gather(bf16[64,1536]{1,0:T(8,128)(2,1)S(1)} %add_convert_fusion), channel_id=1, replica_groups=mesh['groups'=2,'expert'=8,'sub'=2] {'sub'}, dimensions={1}, use_global_device_ids=true | all-gather | bytes 589824 | tf_op jit(solution)/shard_map/all_gather | solution.py:108
  35.7 1.0 gather_fusion.4
  37.5 0.8 collective-permute-start.13
  38.3 1.0 collective-permute-start.12
  39.3 1.4 %collective-permute-start.11 = (bf16[17]{0:T(256)(128)(2,1)S(1)}, bf16[17]{0:T(256)(128)(2,1)S(1)}, u32[]{:S(2)}, u32[]{:S(2)}) collective-permute-start(bf16[17]{0:T(256)(128)(2,1)S(1)} %get-tuple-element.14), channel_id=1, source_target_pairs={{0,10},{2,12},{4,14},{6,0},{8,2},{10,4},{12,6},{14,8},{1,11},{3,13... | collective-permute-start | bytes 110 | tf_op jit(solution)/shard_map/ppermute | solution.py:29
  40.7 1.8 %collective-permute-start.10 = (bf16[17]{0:T(256)(128)(2,1)S(1)}, bf16[17]{0:T(256)(128)(2,1)S(1)}, u32[]{:S(2)}, u32[]{:S(2)}) collective-permute-start(bf16[17]{0:T(256)(128)(2,1)S(1)} %get-tuple-element.15), channel_id=1, source_target_pairs={{0,8},{2,10},{4,12},{6,14},{8,0},{10,2},{12,4},{14,6},{1,9},{3,11}... | collective-permute-start | bytes 110 | tf_op jit(solution)/shard_map/ppermute | solution.py:29
  42.5 1.3 %collective-permute-start.9 = (bf16[17]{0:T(256)(128)(2,1)S(1)}, bf16[17]{0:T(256)(128)(2,1)S(1)}, u32[]{:S(2)}, u32[]{:S(2)}) collective-permute-start(bf16[17]{0:T(256)(128)(2,1)S(1)} %get-tuple-element.16), channel_id=1, source_target_pairs={{0,6},{2,8},{4,10},{6,12},{8,14},{10,0},{12,2},{14,4},{1,7},{3,9},... | collective-permute-start | bytes 110 | tf_op jit(solution)/shard_map/ppermute | solution.py:29
  43.8 0.6 convolution_convert_fusion
  44.5 1.8 %collective-permute-start.8 = (bf16[17]{0:T(256)(128)(2,1)S(1)}, bf16[17]{0:T(256)(128)(2,1)S(1)}, u32[]{:S(2)}, u32[]{:S(2)}) collective-permute-start(bf16[17]{0:T(256)(128)(2,1)S(1)} %get-tuple-element.17), channel_id=1, source_target_pairs={{0,4},{2,6},{4,8},{6,10},{8,12},{10,14},{12,0},{14,2},{1,5},{3,7},... | collective-permute-start | bytes 110 | tf_op jit(solution)/shard_map/ppermute | solution.py:29
  46.7 4.3 %collective-permute-start.6 = (bf16[17,3072]{1,0:T(8,128)(2,1)S(1)}, bf16[17,3072]{1,0:T(8,128)(2,1)S(1)}, u32[]{:S(2)}, u32[]{:S(2)}) collective-permute-start(bf16[17,3072]{1,0:T(8,128)(2,1)S(1)} %get-tuple-element.2), channel_id=1, source_target_pairs={{0,14},{2,0},{4,2},{6,4},{8,6},{10,8},{12,10},{14,12},{1,15},{3,1}... | collective-permute-start | bytes 313352 | tf_op jit(solution)/shard_map/ppermute | solution.py:29
  51.4 2.7 %collective-permute-start.3 = (bf16[17,3072]{1,0:T(8,128)(2,1)S(1)}, bf16[17,3072]{1,0:T(8,128)(2,1)S(1)}, u32[]{:S(2)}, u32[]{:S(2)}) collective-permute-start(bf16[17,3072]{1,0:T(8,128)(2,1)S(1)} %get-tuple-element.5), channel_id=1, source_target_pairs={{0,8},{2,10},{4,12},{6,14},{8,0},{10,2},{12,4},{14,6},{1,9},{3,11}... | collective-permute-start | bytes 313352 | tf_op jit(solution)/shard_map/ppermute | solution.py:29
  54.1 1.9 %collective-permute-start = (bf16[17,3072]{1,0:T(8,128)(2,1)S(1)}, bf16[17,3072]{1,0:T(8,128)(2,1)S(1)}, u32[]{:S(2)}, u32[]{:S(2)}) collective-permute-start(bf16[17,3072]{1,0:T(8,128)(2,1)S(1)} %get-tuple-element.8), channel_id=1, source_target_pairs={{0,2},{2,4},{4,6},{6,8},{8,10},{10,12},{12,14},{14,0},{1,3},{3,5},... | collective-permute-start | bytes 313352 | tf_op jit(solution)/shard_map/ppermute | solution.py:29
  56.8 6.5 %collective-permute-done = bf16[17,3072]{1,0:T(8,128)(2,1)S(1)} collective-permute-done((bf16[17,3072]{1,0:T(8,128)(2,1)S(1)}, bf16[17,3072]{1,0:T(8,128)(2,1)S(1)}, u32[]{:S(2)}, u32[]{:S(2)}) %collective-permute-start) | collective-permute-done | bytes 104480 | tf_op jit(solution)/shard_map/ppermute | solution.py:29
  63.3 1.5 %collective-permute-start.1 = (bf16[17,3072]{1,0:T(8,128)(2,1)S(1)}, bf16[17,3072]{1,0:T(8,128)(2,1)S(1)}, u32[]{:S(2)}, u32[]{:S(2)}) collective-permute-start(bf16[17,3072]{1,0:T(8,128)(2,1)S(1)} %get-tuple-element.7), channel_id=1, source_target_pairs={{0,4},{2,6},{4,8},{6,10},{8,12},{10,14},{12,0},{14,2},{1,5},{3,7},... | collective-permute-start | bytes 313352 | tf_op jit(solution)/shard_map/ppermute | solution.py:29
  64.9 6.0 %collective-permute-done.1 = bf16[17,3072]{1,0:T(8,128)(2,1)S(1)} collective-permute-done((bf16[17,3072]{1,0:T(8,128)(2,1)S(1)}, bf16[17,3072]{1,0:T(8,128)(2,1)S(1)}, u32[]{:S(2)}, u32[]{:S(2)}) %collective-permute-start.1) | collective-permute-done | bytes 104480 | tf_op jit(solution)/shard_map/ppermute | solution.py:29
  70.9 1.6 %collective-permute-start.2 = (bf16[17,3072]{1,0:T(8,128)(2,1)S(1)}, bf16[17,3072]{1,0:T(8,128)(2,1)S(1)}, u32[]{:S(2)}, u32[]{:S(2)}) collective-permute-start(bf16[17,3072]{1,0:T(8,128)(2,1)S(1)} %get-tuple-element.6), channel_id=1, source_target_pairs={{0,6},{2,8},{4,10},{6,12},{8,14},{10,0},{12,2},{14,4},{1,7},{3,9},... | collective-permute-start | bytes 313352 | tf_op jit(solution)/shard_map/ppermute | solution.py:29
  72.5 8.5 %collective-permute-done.2 = bf16[17,3072]{1,0:T(8,128)(2,1)S(1)} collective-permute-done((bf16[17,3072]{1,0:T(8,128)(2,1)S(1)}, bf16[17,3072]{1,0:T(8,128)(2,1)S(1)}, u32[]{:S(2)}, u32[]{:S(2)}) %collective-permute-start.2) | collective-permute-done | bytes 104480 | tf_op jit(solution)/shard_map/ppermute | solution.py:29
  82.3 10.1 %fusion.3 = f32[136,4096]{1,0:T(8,128)S(1)} fusion(bf16[136,3072]{1,0:T(8,128)(2,1)S(1)} %select_n.256, bf16[2,3072,4096]{2,1,0:T(8,128)(2,1)} %param.19), kind=kOutput, calls=%fused_computation.8 | convolution fusion | flops 3422552064 | bytes 28229632 | tf_op jit(solution)/shard_map/dot_general | solution.py:154
  92.4 11.3 %fusion.13 = bf16[136,4096]{1,0:T(8,128)(2,1)} fusion(bf16[136,3072]{1,0:T(8,128)(2,1)S(1)} %select_n.256, bf16[2,3072,4096]{2,1,0:T(8,128)(2,1)} %param.19, f32[136,4096]{1,0:T(8,128)S(1)} %fusion.3, f32[136]{0:T(256)S(1)} %select_n.260), kind=kOutput, calls=%fused_computation.14 | convolution fusion | flops 3426451456 | bytes 29344288 | tf_op jit(solution)/shard_map/dot_general | solution.py:155
  (99 shorter events, 8.1 us)
Async XLA Ops:
  0.6 34.7 %copy-start = (bf16[3072,8]{0,1:T(8,128)(2,1)S(1)}, bf16[3072,8]{0,1:T(8,128)(2,1)}, u32[]{:S(2)}) copy-start(bf16[3072,8]{0,1:T(8,128)(2,1)} %param.17) | copy-start | bytes 147460
  0.6 21.9 %copy-start.2 = (bf16[64,1536]{1,0:T(8,128)(2,1)S(1)}, bf16[64,1536]{1,0:T(8,128)(2,1)}, u32[]{:S(2)}) copy-start(bf16[64,1536]{1,0:T(8,128)(2,1)} %param.11) | copy-start | bytes 589828
  0.7 29.2 %copy-start.4 = (bf16[2,64,512]{2,1,0:T(8,128)(2,1)S(1)}, bf16[2,64,512]{2,1,0:T(8,128)(2,1)}, u32[]{:S(2)}) copy-start(bf16[2,64,512]{2,1,0:T(8,128)(2,1)} %param.12) | copy-start | bytes 393220
  2.2 13.7 %all-to-all-start = ((s32[8,1,1]{2,1,0:T(1,128)}), s32[8,1,1]{2,1,0:T(1,128)S(1)}, u32[]{:S(2)}, u32[]{:S(2)}) async-start(s32[8,1,1]{2,1,0:T(1,128)} %copy.83), calls=%async_computation | async-start | bytes 8192 | tf_op jit(solution)/shard_map/all_to_all | solution.py:98
  18.9 10.2 %all-to-all-start.1 = ((bf16[2,8,4,512]{3,2,0,1:T(4,128)(2,1)}), bf16[2,8,4,512]{3,2,0,1:T(4,128)(2,1)S(1)}, u32[]{:S(2)}, u32[]{:S(2)}) async-start(bf16[2,8,4,512]{3,2,0,1:T(4,128)(2,1)} %select_bitcast_fusion), calls=%async_computation.1 | async-start | bytes 131072 | tf_op jit(solution)/shard_map/all_to_all | solution.py:100
  32.1 0.9 copy-start.3
  32.4 3.0 %copy-start.5 = (f32[3072]{0:T(1024)S(1)}, f32[3072]{0:T(1024)}, u32[]{:S(2)}) copy-start(f32[3072]{0:T(1024)} %param.16) | copy-start | bytes 36868
  33.1 3.6 %copy-start.1 = (bf16[64,1536]{1,0:T(8,128)(2,1)}, bf16[64,1536]{1,0:T(8,128)(2,1)S(1)}, u32[]{:S(2)}) copy-start(bf16[64,1536]{1,0:T(8,128)(2,1)S(1)} %add_convert_fusion) | copy-start | bytes 589828
  35.7 1.3 %copy-start.6 = (s32[64,2]{0,1:T(2,128)S(1)}, s32[64,2]{0,1:T(2,128)}, u32[]{:S(2)}) copy-start(s32[64,2]{0,1:T(2,128)} %param.18) | copy-start | bytes 1540
  37.5 7.0 %collective-permute-start.13 = (bf16[17]{0:T(256)(128)(2,1)S(1)}, bf16[17]{0:T(256)(128)(2,1)S(1)}, u32[]{:S(2)}, u32[]{:S(2)}) collective-permute-start(bf16[17]{0:T(256)(128)(2,1)S(1)} %get-tuple-element.12), channel_id=1, source_target_pairs={{0,14},{2,0},{4,2},{6,4},{8,6},{10,8},{12,10},{14,12},{1,15},{3,1}... | collective-permute-start | bytes 110 | tf_op jit(solution)/shard_map/ppermute | solution.py:29
  38.3 8.0 %collective-permute-start.12 = (bf16[17]{0:T(256)(128)(2,1)S(1)}, bf16[17]{0:T(256)(128)(2,1)S(1)}, u32[]{:S(2)}, u32[]{:S(2)}) collective-permute-start(bf16[17]{0:T(256)(128)(2,1)S(1)} %get-tuple-element.13), channel_id=1, source_target_pairs={{0,12},{2,14},{4,0},{6,2},{8,4},{10,6},{12,8},{14,10},{1,13},{3,15... | collective-permute-start | bytes 110 | tf_op jit(solution)/shard_map/ppermute | solution.py:29
  39.3 7.4 %collective-permute-start.11 = (bf16[17]{0:T(256)(128)(2,1)S(1)}, bf16[17]{0:T(256)(128)(2,1)S(1)}, u32[]{:S(2)}, u32[]{:S(2)}) collective-permute-start(bf16[17]{0:T(256)(128)(2,1)S(1)} %get-tuple-element.14), channel_id=1, source_target_pairs={{0,10},{2,12},{4,14},{6,0},{8,2},{10,4},{12,6},{14,8},{1,11},{3,13... | collective-permute-start | bytes 110 | tf_op jit(solution)/shard_map/ppermute | solution.py:29
  40.7 10.4 %collective-permute-start.10 = (bf16[17]{0:T(256)(128)(2,1)S(1)}, bf16[17]{0:T(256)(128)(2,1)S(1)}, u32[]{:S(2)}, u32[]{:S(2)}) collective-permute-start(bf16[17]{0:T(256)(128)(2,1)S(1)} %get-tuple-element.15), channel_id=1, source_target_pairs={{0,8},{2,10},{4,12},{6,14},{8,0},{10,2},{12,4},{14,6},{1,9},{3,11}... | collective-permute-start | bytes 110 | tf_op jit(solution)/shard_map/ppermute | solution.py:29
  42.5 8.9 %collective-permute-start.9 = (bf16[17]{0:T(256)(128)(2,1)S(1)}, bf16[17]{0:T(256)(128)(2,1)S(1)}, u32[]{:S(2)}, u32[]{:S(2)}) collective-permute-start(bf16[17]{0:T(256)(128)(2,1)S(1)} %get-tuple-element.16), channel_id=1, source_target_pairs={{0,6},{2,8},{4,10},{6,12},{8,14},{10,0},{12,2},{14,4},{1,7},{3,9},... | collective-permute-start | bytes 110 | tf_op jit(solution)/shard_map/ppermute | solution.py:29
  44.5 6.8 %collective-permute-start.8 = (bf16[17]{0:T(256)(128)(2,1)S(1)}, bf16[17]{0:T(256)(128)(2,1)S(1)}, u32[]{:S(2)}, u32[]{:S(2)}) collective-permute-start(bf16[17]{0:T(256)(128)(2,1)S(1)} %get-tuple-element.17), channel_id=1, source_target_pairs={{0,4},{2,6},{4,8},{6,10},{8,12},{10,14},{12,0},{14,2},{1,5},{3,7},... | collective-permute-start | bytes 110 | tf_op jit(solution)/shard_map/ppermute | solution.py:29
  46.3 7.8 %collective-permute-start.7 = (bf16[17]{0:T(256)(128)(2,1)S(1)}, bf16[17]{0:T(256)(128)(2,1)S(1)}, u32[]{:S(2)}, u32[]{:S(2)}) collective-permute-start(bf16[17]{0:T(256)(128)(2,1)S(1)} %get-tuple-element.18), channel_id=1, source_target_pairs={{0,2},{2,4},{4,6},{6,8},{8,10},{10,12},{12,14},{14,0},{1,3},{3,5},... | collective-permute-start | bytes 110 | tf_op jit(solution)/shard_map/ppermute | solution.py:29
  46.7 34.4 %collective-permute-start.6 = (bf16[17,3072]{1,0:T(8,128)(2,1)S(1)}, bf16[17,3072]{1,0:T(8,128)(2,1)S(1)}, u32[]{:S(2)}, u32[]{:S(2)}) collective-permute-start(bf16[17,3072]{1,0:T(8,128)(2,1)S(1)} %get-tuple-element.2), channel_id=1, source_target_pairs={{0,14},{2,0},{4,2},{6,4},{8,6},{10,8},{12,10},{14,12},{1,15},{3,1}... | collective-permute-start | bytes 313352 | tf_op jit(solution)/shard_map/ppermute | solution.py:29
  51.1 30.0 %collective-permute-start.5 = (bf16[17,3072]{1,0:T(8,128)(2,1)S(1)}, bf16[17,3072]{1,0:T(8,128)(2,1)S(1)}, u32[]{:S(2)}, u32[]{:S(2)}) collective-permute-start(bf16[17,3072]{1,0:T(8,128)(2,1)S(1)} %get-tuple-element.3), channel_id=1, source_target_pairs={{0,12},{2,14},{4,0},{6,2},{8,4},{10,6},{12,8},{14,10},{1,13},{3,15... | collective-permute-start | bytes 313352 | tf_op jit(solution)/shard_map/ppermute | solution.py:29
  51.4 29.7 %collective-permute-start.4 = (bf16[17,3072]{1,0:T(8,128)(2,1)S(1)}, bf16[17,3072]{1,0:T(8,128)(2,1)S(1)}, u32[]{:S(2)}, u32[]{:S(2)}) collective-permute-start(bf16[17,3072]{1,0:T(8,128)(2,1)S(1)} %get-tuple-element.4), channel_id=1, source_target_pairs={{0,10},{2,12},{4,14},{6,0},{8,2},{10,4},{12,6},{14,8},{1,11},{3,13... | collective-permute-start | bytes 313352 | tf_op jit(solution)/shard_map/ppermute | solution.py:29
  51.4 29.6 %collective-permute-start.3 = (bf16[17,3072]{1,0:T(8,128)(2,1)S(1)}, bf16[17,3072]{1,0:T(8,128)(2,1)S(1)}, u32[]{:S(2)}, u32[]{:S(2)}) collective-permute-start(bf16[17,3072]{1,0:T(8,128)(2,1)S(1)} %get-tuple-element.5), channel_id=1, source_target_pairs={{0,8},{2,10},{4,12},{6,14},{8,0},{10,2},{12,4},{14,6},{1,9},{3,11}... | collective-permute-start | bytes 313352 | tf_op jit(solution)/shard_map/ppermute | solution.py:29
  54.1 9.2 %collective-permute-start = (bf16[17,3072]{1,0:T(8,128)(2,1)S(1)}, bf16[17,3072]{1,0:T(8,128)(2,1)S(1)}, u32[]{:S(2)}, u32[]{:S(2)}) collective-permute-start(bf16[17,3072]{1,0:T(8,128)(2,1)S(1)} %get-tuple-element.8), channel_id=1, source_target_pairs={{0,2},{2,4},{4,6},{6,8},{8,10},{10,12},{12,14},{14,0},{1,3},{3,5},... | collective-permute-start | bytes 313352 | tf_op jit(solution)/shard_map/ppermute | solution.py:29
  63.3 7.6 %collective-permute-start.1 = (bf16[17,3072]{1,0:T(8,128)(2,1)S(1)}, bf16[17,3072]{1,0:T(8,128)(2,1)S(1)}, u32[]{:S(2)}, u32[]{:S(2)}) collective-permute-start(bf16[17,3072]{1,0:T(8,128)(2,1)S(1)} %get-tuple-element.7), channel_id=1, source_target_pairs={{0,4},{2,6},{4,8},{6,10},{8,12},{10,14},{12,0},{14,2},{1,5},{3,7},... | collective-permute-start | bytes 313352 | tf_op jit(solution)/shard_map/ppermute | solution.py:29
  70.9 10.1 %collective-permute-start.2 = (bf16[17,3072]{1,0:T(8,128)(2,1)S(1)}, bf16[17,3072]{1,0:T(8,128)(2,1)S(1)}, u32[]{:S(2)}, u32[]{:S(2)}) collective-permute-start(bf16[17,3072]{1,0:T(8,128)(2,1)S(1)} %get-tuple-element.6), channel_id=1, source_target_pairs={{0,6},{2,8},{4,10},{6,12},{8,14},{10,0},{12,2},{14,4},{1,7},{3,9},... | collective-permute-start | bytes 313352 | tf_op jit(solution)/shard_map/ppermute | solution.py:29
where the time goes:
time: 104 us
  starting transfers between devices  31.5 us (30%)
  waiting for transfers between devices  30.2 us (29%)
  matrix products  24.5 us (24%)
  local copies, waits for them, and re-layouts  8.52 us (8%)
  other arithmetic  5 us (5%)
  blocking collectives  2.09 us (2%)
  between operations  1.83 us (2%)
    ppermute x14, waiting for transfers between devices, from_behind(): return lax.ppermute(value, axis, pairs)  21.1 us
    ppermute x14, starting transfers between devices, from_behind(): return lax.ppermute(value, axis, pairs)  20.8 us
    dot_general x1, matrix products, shards(): up_part = jnp.dot(slot_rows, w_in[1], preferred_element_type=jnp.float32)  11.3 us
    dot_general x1, matrix products, shards(): gate_part = jnp.dot(slot_rows, w_in[0], preferred_element_type=jnp.float32)  10.1 us
    all_to_all x1, starting transfers between devices, shards(): lax.all_to_all(wanted[:, None], 'expert', split_axis=0, concat_axis=0, ti...  7.28 us
    all_to_all x1, waiting for transfers between devices, shards(): lax.all_to_all(served, 'expert', split_axis=1, concat_axis=1, tiled=True)  6.13 us
    all_to_all x1, starting transfers between devices, shards(): lax.all_to_all(served, 'expert', split_axis=1, concat_axis=1, tiled=True)  3.35 us
    all_to_all x1, waiting for transfers between devices, shards(): lax.all_to_all(wanted[:, None], 'expert', split_axis=0, concat_axis=0, ti...  2.95 us
  transfers between devices with their start and end apart: 16, of which 5 were waited for; matrix products, arithmetic and copies ran while one was open for 5% of the time, Pallas kernels for 0%

commit v1 on v0

v1 whole, which is shorter than its diff:
```python
import math

import jax
import jax.numpy as jnp
from jax import lax
from jax.experimental import pallas as pl
from jax.experimental.pallas import tpu as pltpu
from jax.sharding import PartitionSpec as P

HEAD_WIDTH = 128
EXPERTS = 8
TOP = 2
CAP = 17
LANES = 128
MIB = 1 << 20
FIRST = (0, 3)
BF16 = jnp.bfloat16
F32 = jnp.float32


def swap(array, axis, bit):
    return lax.ppermute(array, axis, [(i, i ^ (1 << bit)) for i in range(lax.axis_size(axis))])


def from_behind(array, axis, steps):
    count = lax.axis_size(axis)
    return lax.ppermute(array, axis, [(i, (i + steps) % count) for i in range(count)])


def mm(a, b):
    return jnp.dot(a, b, preferred_element_type=F32)


def mm_t(a, b):
    return lax.dot_general(a, b, (((1,), (1,)), ((), ())), preferred_element_type=F32)


def attend_kernel(q_ref, new_ref, pages_ref, hot_ref, plen_ref, in_ref, pick_ref, noted_ref,
                  stream_ref, out_refs):
    tokens = q_ref.shape[0]
    kv_heads = new_ref.shape[2] // HEAD_WIDTH
    grouped = q_ref.shape[1] // HEAD_WIDTH // kv_heads
    prefix = hot_ref.shape[0]
    pages = pages_ref[...].astype(F32)
    width = new_ref.shape[2]
    hot = hot_ref[...]
    keys_p = mm(hot, pages[:, 0].reshape(-1, width).astype(BF16)).astype(BF16)
    vals_p = mm(hot, pages[:, 1].reshape(-1, width).astype(BF16)).astype(BF16)
    rows = grouped * tokens
    live_p = lax.broadcasted_iota(jnp.int32, (rows, prefix), 1) < plen_ref[0]
    at = lax.broadcasted_iota(jnp.int32, (rows, tokens), 0) % tokens
    live_n = lax.broadcasted_iota(jnp.int32, (rows, tokens), 1) <= at
    factor = 1.0 / math.sqrt(HEAD_WIDTH)
    for k in range(kv_heads):
        cols = pl.ds(k * HEAD_WIDTH, HEAD_WIDTH)
        sl = slice(k * HEAD_WIDTH, (k + 1) * HEAD_WIDTH)
        heads = [k * grouped + g for g in range(grouped)]
        q = jnp.concatenate(
            [q_ref[:, h * HEAD_WIDTH : (h + 1) * HEAD_WIDTH] for h in heads], axis=0
        )
        s_p = jnp.where(live_p, mm_t(q, keys_p[:, sl]) * factor, -1e30)
        s_n = jnp.where(live_n, mm_t(q, new_ref[0, :, cols]) * factor, -1e30)
        top = jnp.maximum(
            jnp.max(s_p, axis=-1, keepdims=True), jnp.max(s_n, axis=-1, keepdims=True)
        )
        e_p = jnp.exp(s_p - top)
        e_n = jnp.exp(s_n - top)
        total = jnp.sum(e_p, axis=-1, keepdims=True) + jnp.sum(e_n, axis=-1, keepdims=True)
        w_p = (e_p / total).astype(BF16)
        w_n = (e_n / total).astype(BF16)
        mixed = (mm(w_p, vals_p[:, sl]) + mm(w_n, new_ref[1, :, cols])).astype(BF16)
        for g, h in enumerate(heads):
            hs = slice(h * HEAD_WIDTH, (h + 1) * HEAD_WIDTH)
            part = mixed[g * tokens : (g + 1) * tokens].astype(F32)
            stream_ref[:, hs] = (in_ref[:, hs].astype(F32) + part).astype(BF16)
    sent = mm(pick_ref[...], stream_ref[...])
    width = stream_ref.shape[1]
    padded = sent.shape[0] // EXPERTS
    folds = width // LANES
    spare = CAP - 1 - folds - 1
    for e, out_ref in enumerate(out_refs):
        first = e * padded
        out_ref[:, :width] = sent[first : first + CAP - 1].astype(BF16)
        last = sent[first + CAP - 1 : first + CAP]
        lines = [last[:, c * LANES : (c + 1) * LANES] for c in range(folds)]
        lines += [noted_ref[e : e + 1, :], jnp.zeros((spare, LANES), F32)]
        out_ref[:, width:] = jnp.concatenate(lines, axis=0).astype(BF16)


def attend(queries, kv_new, pages, hot, prefix_len, stream_in, pick, noted, marks):
    tokens, width = stream_in.shape
    vm = pl.BlockSpec(memory_space=pltpu.VMEM)

    def body(*refs):
        inputs = refs[:8]
        outputs = refs[8 + len(marks) :]
        attend_kernel(*inputs, outputs[0], outputs[1:])

    return pl.pallas_call(
        body,
        out_shape=[jax.ShapeDtypeStruct((tokens, width), BF16)]
        + [jax.ShapeDtypeStruct((CAP - 1, width + LANES), BF16)] * EXPERTS,
        in_specs=[vm, vm, vm, vm, pl.BlockSpec(memory_space=pltpu.SMEM), vm, vm, vm]
        + [vm] * len(marks),
        out_specs=[vm] * (1 + EXPERTS),
        compiler_params=pltpu.CompilerParams(vmem_limit_bytes=8 * MIB),
        name="attend",
    )(queries, kv_new, pages, hot, prefix_len, stream_in, pick, noted, *marks)


def assemble(parts, marks, group_width):
    width = parts[0].shape[1] - LANES
    slots = EXPERTS * CAP
    padded = -(-CAP // 8) * 8

    def body(*refs):
        home = lax.axis_index("expert") // group_width
        rows_ref, code_ref = refs[EXPERTS + len(marks) :]
        stacked, codes = [], []
        for ref in refs[:EXPERTS]:
            extra = ref[:, width:].astype(F32)
            stacked.append(ref[:, :width].astype(F32))
            lines = [extra[c : c + 1] for c in range(width // LANES)]
            stacked.append(jnp.concatenate(lines, axis=1))
            stacked.append(jnp.zeros((padded - CAP, width), F32))
            codes.append(extra[width // LANES : width // LANES + 1])
        whole = jnp.concatenate(stacked, axis=0).astype(BF16)
        slot = lax.broadcasted_iota(jnp.int32, (slots, padded * EXPERTS), 0)
        column = lax.broadcasted_iota(jnp.int32, (slots, padded * EXPERTS), 1)
        stride = (home - slot // CAP + EXPERTS) % EXPERTS
        order = (column == stride * padded + slot % CAP).astype(F32).astype(BF16)
        rows_ref[...] = mm(order, whole).astype(BF16)
        slot = lax.broadcasted_iota(jnp.int32, (slots, LANES), 0)
        lane = lax.broadcasted_iota(jnp.int32, (slots, LANES), 1)
        stride = (home - slot // CAP + EXPERTS) % EXPERTS
        code = jnp.zeros((slots, 1), F32)
        for k in range(EXPERTS):
            wanted = (lane == slot % CAP) & (stride == k)
            code += jnp.sum(jnp.where(wanted, codes[k], 0.0), axis=1, keepdims=True)
        code_ref[...] = jnp.broadcast_to(code, (slots, LANES)).astype(BF16)

    vm = pl.BlockSpec(memory_space=pltpu.VMEM)
    return pl.pallas_call(
        body,
        out_shape=(
            jax.ShapeDtypeStruct((slots, width), BF16),
            jax.ShapeDtypeStruct((slots, LANES), BF16),
        ),
        in_specs=[vm] * (EXPERTS + len(marks)),
        out_specs=(vm, vm),
        compiler_params=pltpu.CompilerParams(vmem_limit_bytes=8 * MIB),
        name="assemble",
    )(*parts, *marks)


def preload(w_in, first, count, after, name):
    depth = w_in.shape[1]

    def body(w_ref, *refs):
        o_ref, done_ref, sem = refs[len(after) :]
        copy = pltpu.make_async_copy(w_ref.at[:, :, pl.ds(first, count)], o_ref, sem)
        copy.start()
        done_ref[...] = jnp.zeros_like(done_ref)
        copy.wait()

    anywhere = pl.BlockSpec(memory_space=pl.ANY)
    return pl.pallas_call(
        body,
        out_shape=(
            pltpu.VMEM((2, depth, count), BF16),
            jax.ShapeDtypeStruct((8, LANES), F32),
        ),
        in_specs=[anywhere] * (1 + len(after)),
        out_specs=(pl.BlockSpec(memory_space=pltpu.VMEM), pl.BlockSpec(memory_space=pltpu.VMEM)),
        scratch_shapes=[pltpu.SemaphoreType.DMA],
        compiler_params=pltpu.CompilerParams(vmem_limit_bytes=MIB),
        cost_estimate=pl.CostEstimate(
            flops=0, transcendentals=0, bytes_accessed=4 * depth * count
        ),
        name=name,
    )(w_in, *after)


def experts(own, other, code, group_width, gain, router, w_in, held):
    slots = own.shape[0]
    half = own.shape[1]
    depth = 2 * half
    columns = w_in.shape[2]
    held_columns = [h.shape[2] for h in held]
    rest = columns - sum(held_columns)
    start_rest = sum(held_columns)
    block = next(b for b in (256, 128) if all(c % b == 0 for c in [rest] + held_columns))
    pieces = rest // block
    ring = min(pieces, 3)

    def body(*refs):
        own_ref, other_ref, code_ref, gain_ref, router_ref, w_ref = refs[:6]
        held_refs = refs[6 : 6 + len(held)]
        out_ref, rest_ref, normed_ref, sems = refs[6 + len(held) :]

        def fetch(i):
            return pltpu.make_async_copy(
                w_ref.at[:, :, pl.ds(start_rest + i * block, block)],
                rest_ref.at[i % ring],
                sems.at[i % ring],
            )

        for i in range(ring):
            fetch(i).start()
        first = lax.axis_index("sub") == 0
        mine = own_ref[...]
        theirs = other_ref[...]
        low = jnp.where(first, mine, theirs).astype(F32)
        high = jnp.where(first, theirs, mine).astype(F32)
        square = jnp.sum(low * low, axis=1, keepdims=True) + jnp.sum(
            high * high, axis=1, keepdims=True
        )
        scale = lax.rsqrt(square * (1.0 / depth) + 1e-05)
        normed_ref[:, :half] = (low * scale * gain_ref[:, :half]).astype(BF16)
        normed_ref[:, half:] = (high * scale * gain_ref[:, half:]).astype(BF16)
        logits = mm_t(normed_ref[...], router_ref[...])
        here = lax.axis_index("expert") // group_width
        code = code_ref[...].astype(F32)[:, :1].astype(jnp.int32)
        away = code - 1 - here
        lane = lax.broadcasted_iota(jnp.int32, logits.shape, 1)
        mine_logit = jnp.sum(jnp.where(lane == here, logits, 0.0), axis=1, keepdims=True)
        away_logit = jnp.sum(jnp.where(lane == away, logits, 0.0), axis=1, keepdims=True)
        share = 1.0 / (1.0 + jnp.exp(away_logit - mine_logit))
        share = jnp.where(code > 0, share, 0.0)

        def hidden(gate_w, up_w):
            rows = normed_ref[...]
            gate = mm(rows, gate_w)
            up = mm(rows, up_w)
            return (gate / (1.0 + jnp.exp(-gate)) * up * share).astype(BF16)

        def rest_block(i):
            fetch(i).wait()
            at = start_rest + i * block
            out_ref[:, at : at + block] = hidden(rest_ref[i % ring, 0], rest_ref[i % ring, 1])
            if i + ring < pieces:
                fetch(i + ring).start()

        kept = [
            (h_ref, i)
            for h_ref, count in zip(held_refs, held_columns)
            for i in range(count // block)
        ]
        spacing = max(len(kept) // pieces, 1)
        done = 0
        for n in range(len(kept)):
            h_ref, i = kept[n]
            at = slice(i * block, (i + 1) * block)
            out_ref[:, n * block : (n + 1) * block] = hidden(h_ref[0, :, at], h_ref[1, :, at])
            if (n + 1) % spacing == 0 and done < pieces:
                rest_block(done)
                done += 1
        for i in range(done, pieces):
            rest_block(i)

    vm = pl.BlockSpec(memory_space=pltpu.VMEM)
    return pl.pallas_call(
        body,
        out_shape=jax.ShapeDtypeStruct((slots, columns), BF16),
        in_specs=[vm, vm, vm, vm, vm,
                  pl.BlockSpec(memory_space=pl.ANY)] + [vm] * len(held),
        out_specs=vm,
        scratch_shapes=[
            pltpu.VMEM((ring, 2, depth, block), BF16),
            pltpu.VMEM((slots, depth), BF16),
            pltpu.SemaphoreType.DMA((ring,)),
        ],
        compiler_params=pltpu.CompilerParams(
            vmem_limit_bytes=(60 if not held else 17) * MIB
        ),
        name="experts",
    )(own, other, code, gain, router, w_in, *held)


def shards(stream_in, queries, kv_new, paged_key_value_cache, page_table, prefix_len, norm_gain,
           w_router, expert_ids, w_in):
    expert_count = lax.axis_size("expert")
    group_width = expert_count // EXPERTS
    level_values = group_width.bit_length() - 1
    own_index = lax.axis_index("expert")
    own_group = own_index // group_width
    tokens, half = stream_in.shape
    cache = paged_key_value_cache
    page_rows = cache.shape[2]
    shard_rows = cache.shape[1] * page_rows
    columns = w_in.shape[2]
    step = columns // 8 // LANES * LANES

    mine = cache.reshape(1, 2, shard_rows, cache.shape[3])
    pages = lax.all_to_all(
        jnp.broadcast_to(mine, (expert_count,) + mine.shape[1:]), "expert", 0, 0, tiled=True
    )
    early, late = FIRST
    held, marks = [], []
    wanted = (
        page_table[0][:, None] * page_rows + jnp.arange(page_rows, dtype=jnp.int32)[None, :]
    ).reshape(-1, 1)
    hot = (
        wanted == jnp.arange(expert_count * shard_rows, dtype=jnp.int32)[None, :]
    ).astype(BF16)

    named = jnp.sum(
        (expert_ids[:, :, None] == jnp.arange(EXPERTS, dtype=jnp.int32)).astype(jnp.int32), axis=1
    )
    rank = jnp.cumsum(named, axis=0) - named
    slot = jnp.where(named > 0, rank, -1).T
    towards = (own_group + jnp.arange(EXPERTS, dtype=jnp.int32)) % EXPERTS
    slot = jnp.take(slot, towards, axis=0)
    padded = -(-CAP // 16) * 16
    pick = (
        (slot[:, None, :] == jnp.arange(padded, dtype=jnp.int32)[None, :, None])
        .astype(BF16)
        .reshape(EXPERTS * padded, tokens)
    )
    total = jnp.sum(expert_ids, axis=1) + 1
    chosen = slot[:, None, :] == jnp.arange(LANES, dtype=jnp.int32)[None, :, None]
    noted = jnp.sum(jnp.where(chosen, total[None, None, :], 0), axis=2).astype(F32)
    if step >= 256 and early:
        kept, mark = preload(w_in, 0, early * step, (hot, pick, noted), "preload_first")
        held.append(kept)
        marks.append(mark)
    stream, *outgoing = attend(
        queries, kv_new, pages, hot, prefix_len, stream_in, pick, noted, marks
    )
    parts = [outgoing[0]] + [
        from_behind(outgoing[k], "expert", k * group_width) for k in range(1, EXPERTS)
    ]
    marks = []
    if step >= 256 and late:
        kept, mark = preload(w_in, early * step, late * step, outgoing[:1], "preload_second")
        held.append(kept)
        marks.append(mark)
    rows, code = assemble(parts, marks, group_width)
    rows, code = rows[None], code[None]
    for bit in range(level_values):
        is_high = (own_index >> bit) % 2 == 1
        rows, code = (
            jnp.concatenate(
                [jnp.where(is_high, there, here), jnp.where(is_high, here, there)], axis=0
            )
            for here, there in ((rows, swap(rows, "expert", bit)), (code, swap(code, "expert", bit)))
        )
    rows = rows.reshape(-1, half)
    code = code.reshape(-1, LANES)
    other = swap(rows, "sub", 0)
    hidden = experts(
        rows, other, code, group_width, norm_gain[None, :], w_router.T, w_in, held
    )
    return (stream, hidden)


def solution(mesh):
    placed = (
        P(("groups", "expert"), "sub"),
        P(("groups", "expert"), "sub"),
        P(None, ("groups", "expert"), "sub"),
        P(None, ("groups", "expert"), None, "sub"),
        P(("groups", "expert"), None),
        P(("groups", "expert")),
        P(),
        P(),
        P(("groups", "expert"), None),
        P(None, None, ("expert", "sub")),
    )
    return jax.shard_map(
        shards,
        mesh=mesh,
        in_specs=placed,
        out_specs=(P(("groups", "expert"), "sub"), P("groups", ("expert", "sub"))),
        check_vma=False,
    )
```

time: 104 us -> 53.3 us (0.51)
  matrix products: 24.5 us -> 0 us
  waiting for transfers between devices: 30.2 us -> 5.87 us
  Pallas kernels: 0 us -> 21.5 us
  starting transfers between devices: 31.5 us -> 16.4 us
  local copies, waits for them, and re-layouts: 8.52 us -> 5.03 us
  other arithmetic: 5 us -> 2.66 us
  blocking collectives: 2.09 us -> 0 us
    dot_general x7 -> x0, matrix products: 24.1 us -> none  [the longest x1 11.3 us: shards(): up_part = jnp.dot(slot_rows, w_in[1], preferred_element_type=jnp.float32)]
    pallas_call x0 -> x4, Pallas kernels: none -> 21.5 us  [the longest x1 13.1 us: experts(): pl.pallas_call(body, out_shape=jax.ShapeDtypeStruct((slots, columns), BF1...]
    ppermute x14 -> x8, waiting for transfers between devices: 21.1 us -> 2.74 us  [the longest x1 1.74 us: swap(): lax.ppermute(array, axis, [(i, i ^ 1 << bit) for i in range(lax.axis_size...]
    ppermute x14 -> x8, starting transfers between devices: 20.8 us -> 9.16 us  [the longest x7 9.09 us: from_behind(): lax.ppermute(array, axis, [(i, (i + steps) % count) for i in range(count)])]
    all_to_all x2 -> x1, waiting for transfers between devices: 9.08 us -> 3.13 us  [shards(): lax.all_to_all(jnp.broadcast_to(mine, (expert_count,) + mine.shape[1:]),...]
    gather x10 -> x1, local copies, waits for them, and re-layouts: 4.62 us -> 0.56 us  [shards(): slot = jnp.take(slot, towards, axis=0)]
    all_to_all x2 -> x1, starting transfers between devices: 10.6 us -> 7.28 us  [shards(): lax.all_to_all(jnp.broadcast_to(mine, (expert_count,) + mine.shape[1:]),...]
    all_gather x1 -> x0, blocking collectives: 2.09 us -> none  [shards(): stream = lax.all_gather(stream_part, 'sub', axis=1, tiled=True)]
  transfers between devices with their start and end apart: 16 -> 9, of which waited for: 5 -> 3; matrix products, arithmetic and copies ran while one was open for 5% -> 7% of each run, Pallas kernels for 0% -> 12%
where the time goes in v1:
time: 53.3 us; the launch traced here: 52.9 us
  Pallas kernels  21.5 us (40%)
  starting transfers between devices  16.4 us (31%)
  waiting for transfers between devices  5.87 us (11%)
  local copies, waits for them, and re-layouts  5.03 us (9%)
  other arithmetic  2.66 us (5%)
  between operations  1.38 us (3%)
    pallas_call x1, Pallas kernels, experts(): pl.pallas_call(body, out_shape=jax.ShapeDtypeStruct((slots, columns), BF1...  13.1 us
    ppermute x7, starting transfers between devices, from_behind(): lax.ppermute(array, axis, [(i, (i + steps) % count) for i in range(count)])  9.09 us
    all_to_all x1, starting transfers between devices, shards(): lax.all_to_all(jnp.broadcast_to(mine, (expert_count,) + mine.shape[1:]),...  7.28 us
    pallas_call x1, Pallas kernels, preload(): pl.pallas_call(body, out_shape=(pltpu.VMEM((2, depth, count), BF16), jax....  6.38 us
    all_to_all x1, waiting for transfers between devices, shards(): lax.all_to_all(jnp.broadcast_to(mine, (expert_count,) + mine.shape[1:]),...  3.13 us
    unnamed x10, local copies, waits for them, and re-layouts  2.76 us
    ppermute x1, waiting for transfers between devices, swap(): lax.ppermute(array, axis, [(i, i ^ 1 << bit) for i in range(lax.axis_size...  1.74 us
    pallas_call x1, Pallas kernels, attend(): pl.pallas_call(body, out_shape=[jax.ShapeDtypeStruct((tokens, width), BF1...  1.66 us
  transfers between devices with their start and end apart: 9, of which 3 were waited for; matrix products, arithmetic and copies ran while one was open for 7% of the time, Pallas kernels for 12%

profile of v1, /device:TPU:0, one launch (start us, length us, event | category | flops | bytes accessed | tf_op | source)
XLA Modules:
  0.0 52.9 jit_solution(9287261423635494625)
XLA Ops:
  0.6 0.7 %broadcast_in_dim.45 = bf16[2,8,512]{2,1,0:T(8,128)(2,1)S(1)} reshape(bf16[2,2,4,512]{3,2,1,0:T(4,128)(2,1)} %param.13) | data formatting | bytes 32768 | tf_op jit(solution)/shard_map/broadcast_in_dim | solution.py:296
  1.4 0.7 %broadcast_in_dim.46 = bf16[8,2,8,512]{3,2,1,0:T(8,128)(2,1)} broadcast(bf16[2,8,512]{2,1,0:T(8,128)(2,1)S(1)} %broadcast_in_dim.45), dimensions={1,2,3} | broadcast | bytes 147456 | tf_op jit(solution)/shard_map/broadcast_in_dim | solution.py:296
  2.0 7.3 %all-to-all-start = ((bf16[8,2,8,512]{3,2,1,0:T(8,128)(2,1)}), bf16[8,2,8,512]{3,2,1,0:T(8,128)(2,1)S(1)}, u32[]{:S(2)}, u32[]{:S(2)}) async-start(bf16[8,2,8,512]{3,2,1,0:T(8,128)(2,1)} %broadcast_in_dim.46), calls=%async_computation | async-start | bytes 262144 | tf_op jit(solution)/shard_map/all_to_all | solution.py:295
  9.3 0.7 %multiply_bitcast_fusion = s32[8]{0:T(128)S(1)} fusion(s32[1,8]{1,0:T(1,128)} %param.14), kind=kLoop, calls=%fused_computation.25 | loop fusion | flops 8 | bytes 64 | tf_op jit(solution)/shard_map/mul | solution.py:301
  10.0 0.7 %convert_reduce_fusion = s32[64,8]{0,1:T(8,128)S(1)} fusion(s32[64,2]{0,1:T(2,128)} %param.18), kind=kLoop, calls=%fused_computation.7 | loop fusion | flops 2560 | bytes 2560 | tf_op jit(solution)/shard_map/reduce_sum | solution.py:307
  10.7 0.7 %reduce_sum.28 = s32[64]{0:T(128)S(1)} reduce(s32[64,2]{0,1:T(2,128)} %param.18, s32[]{:T(128)} %constant.52.clone.1), dimensions={1}, to_apply=%region_2.3 | reduce | flops 64 | bytes 772 | tf_op jit(solution)/shard_map/reduce_sum | solution.py:320
  11.5 0.1 copy.21
  11.6 0.1 reduce_window_sum.11
  11.7 0.6 %gather_fusion = s32[8,64]{1,0:T(8,128)S(1)} fusion(s32[8,64]{1,0:T(8,128)S(1)} %select_bitcast_fusion, s32[1024]{0:T(1024)S(1)} %pad_clamp_fusion), kind=kCustom, calls=%fused_computation | custom fusion | bytes 4128 | tf_op jit(solution)/shard_map/jit(_take)/gather | solution.py:313
  12.3 0.1 broadcast_select_fusion
  12.4 0.2 select_reduce_fusion
  13.2 0.1 add.85
  13.2 0.1 eq.70
  13.3 0.1 fusion.refs_6_
  13.4 0.1 fusion.1.refs_3_
  13.5 3.1 %all-to-all-done.refs_2_ = bf16[8,2,8,512]{3,2,1,0:T(8,128)(2,1)S(1)} async-done(((bf16[8,2,8,512]{3,2,1,0:T(8,128)(2,1)}), bf16[8,2,8,512]{3,2,1,0:T(8,128)(2,1)S(1)}, u32[]{:S(2)}, u32[]{:S(2)}) %all-to-all-start) | async-done | bytes 131104 | tf_op jit(solution)/shard_map/all_to_all | solution.py:295
  16.7 0.9 %copy-done = bf16[64,1536]{1,0:T(8,128)(2,1)S(1)} copy-done((bf16[64,1536]{1,0:T(8,128)(2,1)S(1)}, bf16[64,1536]{1,0:T(8,128)(2,1)}, u32[]{:S(2)}) %copy-start) | copy-done | bytes 196632
  17.6 0.9 %copy-done.1 = bf16[64,1536]{1,0:T(8,128)(2,1)S(1)} copy-done((bf16[64,1536]{1,0:T(8,128)(2,1)S(1)}, bf16[64,1536]{1,0:T(8,128)(2,1)}, u32[]{:S(2)}) %copy-start.1) | copy-done | bytes 196632
  18.5 0.9 %copy-done.2 = bf16[2,64,512]{2,1,0:T(8,128)(2,1)S(1)} copy-done((bf16[2,64,512]{2,1,0:T(8,128)(2,1)S(1)}, bf16[2,64,512]{2,1,0:T(8,128)(2,1)}, u32[]{:S(2)}) %copy-start.2) | copy-done | bytes 131096
  19.4 1.7 %attend.1 = (bf16[64,1536]{1,0:T(8,128)(2,1)}, bf16[16,1664]{1,0:T(8,128)(2,1)S(1)}, bf16[16,1664]{1,0:T(8,128)(2,1)S(1)}, bf16[16,1664]{1,0:T(8,128)(2,1)S(1)},...) custom-call(bf16[64,1536]{1,0:T(8,128)(2,1)S(1)} %copy-done, ...), custom_call_target="tpu_custom_call" | custom-call | tf_op jit(solution)/shard_map/attend/pallas_call | solution.py:99
  21.1 0.2 collective-permute-start
  21.3 1.1 %collective-permute-start.1 = (bf16[16,1664]{1,0:T(8,128)(2,1)S(1)}, bf16[16,1664]{1,0:T(8,128)(2,1)S(1)}, u32[]{:S(2)}, u32[]{:S(2)}) collective-permute-start(bf16[16,1664]{1,0:T(8,128)(2,1)S(1)} %get-tuple-element.18), channel_id=1, source_target_pairs={{0,4},{2,6},{4,8},{6,10},{8,12},{10,14},{12,0},{14,2},{1,5},{3,7},... | collective-permute-start | bytes 159752 | tf_op jit(solution)/shard_map/ppermute | solution.py:27
  22.4 1.4 %collective-permute-start.2 = (bf16[16,1664]{1,0:T(8,128)(2,1)S(1)}, bf16[16,1664]{1,0:T(8,128)(2,1)S(1)}, u32[]{:S(2)}, u32[]{:S(2)}) collective-permute-start(bf16[16,1664]{1,0:T(8,128)(2,1)S(1)} %get-tuple-element.19), channel_id=1, source_target_pairs={{0,6},{2,8},{4,10},{6,12},{8,14},{10,0},{12,2},{14,4},{1,7},{3,9},... | collective-permute-start | bytes 159752 | tf_op jit(solution)/shard_map/ppermute | solution.py:27
  23.8 2.6 %collective-permute-start.3 = (bf16[16,1664]{1,0:T(8,128)(2,1)S(1)}, bf16[16,1664]{1,0:T(8,128)(2,1)S(1)}, u32[]{:S(2)}, u32[]{:S(2)}) collective-permute-start(bf16[16,1664]{1,0:T(8,128)(2,1)S(1)} %get-tuple-element.20), channel_id=1, source_target_pairs={{0,8},{2,10},{4,12},{6,14},{8,0},{10,2},{12,4},{14,6},{1,9},{3,11}... | collective-permute-start | bytes 159752 | tf_op jit(solution)/shard_map/ppermute | solution.py:27
  26.4 1.3 %collective-permute-start.4 = (bf16[16,1664]{1,0:T(8,128)(2,1)S(1)}, bf16[16,1664]{1,0:T(8,128)(2,1)S(1)}, u32[]{:S(2)}, u32[]{:S(2)}) collective-permute-start(bf16[16,1664]{1,0:T(8,128)(2,1)S(1)} %get-tuple-element.21), channel_id=1, source_target_pairs={{0,10},{2,12},{4,14},{6,0},{8,2},{10,4},{12,6},{14,8},{1,11},{3,13... | collective-permute-start | bytes 159752 | tf_op jit(solution)/shard_map/ppermute | solution.py:27
  27.6 1.0 %collective-permute-done.refs_1_ = bf16[16,1664]{1,0:T(8,128)(2,1)S(1)} collective-permute-done((bf16[16,1664]{1,0:T(8,128)(2,1)S(1)}, bf16[16,1664]{1,0:T(8,128)(2,1)S(1)}, u32[]{:S(2)}, u32[]{:S(2)}) %collective-permute-start) | collective-permute-done | bytes 53280 | tf_op jit(solution)/shard_map/ppermute | solution.py:27
  28.6 0.7 %collective-permute-start.5 = (bf16[16,1664]{1,0:T(8,128)(2,1)S(1)}, bf16[16,1664]{1,0:T(8,128)(2,1)S(1)}, u32[]{:S(2)}, u32[]{:S(2)}) collective-permute-start(bf16[16,1664]{1,0:T(8,128)(2,1)S(1)} %get-tuple-element.22), channel_id=1, source_target_pairs={{0,12},{2,14},{4,0},{6,2},{8,4},{10,6},{12,8},{14,10},{1,13},{3,15... | collective-permute-start | bytes 159752 | tf_op jit(solution)/shard_map/ppermute | solution.py:27
  29.3 1.9 %collective-permute-start.6 = (bf16[16,1664]{1,0:T(8,128)(2,1)S(1)}, bf16[16,1664]{1,0:T(8,128)(2,1)S(1)}, u32[]{:S(2)}, u32[]{:S(2)}) collective-permute-start(bf16[16,1664]{1,0:T(8,128)(2,1)S(1)} %get-tuple-element.23), channel_id=1, source_target_pairs={{0,14},{2,0},{4,2},{6,4},{8,6},{10,8},{12,10},{14,12},{1,15},{3,1}... | collective-permute-start | bytes 159752 | tf_op jit(solution)/shard_map/ppermute | solution.py:27
  31.2 6.4 %preload_second.1 = (bf16[2,3072,1536]{2,1,0:T(8,128)(2,1)S(1)}, f32[8,128]{1,0:T(8,128)S(1)}) custom-call(bf16[2,3072,4096]{2,1,0:T(8,128)(2,1)} %refs_5_.3, bf16[16,1664]{1,0:T(8,128)(2,1)S(1)} %get-tuple-element.16.refs_0_), custom_call_target="tpu_custom_call" | custom-call | bytes 18874368 | tf_op jit(solution)/shard_map/preload_second/pallas_call | solution.py:167
  37.6 0.3 assemble.1
  38.0 1.7 %collective-permute-done.7.refs_1_ = bf16[136,1536]{1,0:T(8,128)(2,1)S(1)} collective-permute-done((bf16[136,1536]{1,0:T(8,128)(2,1)S(1)}, bf16[136,1536]{1,0:T(8,128)(2,1)S(1)}, u32[]{:S(2)}, u32[]{:S(2)}) %collective-permute-start.7) | collective-permute-done | bytes 417824 | tf_op jit(solution)/shard_map/ppermute | solution.py:22
  39.8 13.1 %experts.1 = bf16[136,4096]{1,0:T(8,128)(2,1)} custom-call(bf16[136,1536]{1,0:T(8,128)(2,1)S(1)} %get-tuple-element.25.refs_0_, bf16[136,1536]{1,0:T(8,128)(2,1)S(1)} %collective-permute-done.7.refs_1_, bf16[136,128]{1,0:T(8,128)(2,1)S(1)} %get-tuple-element.26.refs_2_, f32[1,3072]{1,0:T(1,128)S(1)} %bitcast.13, bf16[8,3072]{1,0:T(8,128)(2,1)S(1)} %bitcast.12, ...), custom_call_target="tpu_custom_call" | custom-call | tf_op jit(solution)/shard_map/experts/pallas_call | solution.py:262
  (23 shorter events, 0.3 us)
Async XLA Ops:
  2.0 14.6 %all-to-all-start = ((bf16[8,2,8,512]{3,2,1,0:T(8,128)(2,1)}), bf16[8,2,8,512]{3,2,1,0:T(8,128)(2,1)S(1)}, u32[]{:S(2)}, u32[]{:S(2)}) async-start(bf16[8,2,8,512]{3,2,1,0:T(8,128)(2,1)} %broadcast_in_dim.46), calls=%async_computation | async-start | bytes 262144 | tf_op jit(solution)/shard_map/all_to_all | solution.py:295
  16.7 0.9 %copy-start = (bf16[64,1536]{1,0:T(8,128)(2,1)S(1)}, bf16[64,1536]{1,0:T(8,128)(2,1)}, u32[]{:S(2)}) copy-start(bf16[64,1536]{1,0:T(8,128)(2,1)} %refs_0_.1) | copy-start | bytes 589828
  17.6 0.9 %copy-start.1 = (bf16[64,1536]{1,0:T(8,128)(2,1)S(1)}, bf16[64,1536]{1,0:T(8,128)(2,1)}, u32[]{:S(2)}) copy-start(bf16[64,1536]{1,0:T(8,128)(2,1)} %refs_5_.2) | copy-start | bytes 589828
  18.5 0.9 %copy-start.2 = (bf16[2,64,512]{2,1,0:T(8,128)(2,1)S(1)}, bf16[2,64,512]{2,1,0:T(8,128)(2,1)}, u32[]{:S(2)}) copy-start(bf16[2,64,512]{2,1,0:T(8,128)(2,1)} %refs_1_.1) | copy-start | bytes 393220
  21.1 7.5 %collective-permute-start = (bf16[16,1664]{1,0:T(8,128)(2,1)S(1)}, bf16[16,1664]{1,0:T(8,128)(2,1)S(1)}, u32[]{:S(2)}, u32[]{:S(2)}) collective-permute-start(bf16[16,1664]{1,0:T(8,128)(2,1)S(1)} %get-tuple-element.17), channel_id=1, source_target_pairs={{0,2},{2,4},{4,6},{6,8},{8,10},{10,12},{12,14},{14,0},{1,3},{3,5},... | collective-permute-start | bytes 159752 | tf_op jit(solution)/shard_map/ppermute | solution.py:27
  21.3 8.0 %collective-permute-start.1 = (bf16[16,1664]{1,0:T(8,128)(2,1)S(1)}, bf16[16,1664]{1,0:T(8,128)(2,1)S(1)}, u32[]{:S(2)}, u32[]{:S(2)}) collective-permute-start(bf16[16,1664]{1,0:T(8,128)(2,1)S(1)} %get-tuple-element.18), channel_id=1, source_target_pairs={{0,4},{2,6},{4,8},{6,10},{8,12},{10,14},{12,0},{14,2},{1,5},{3,7},... | collective-permute-start | bytes 159752 | tf_op jit(solution)/shard_map/ppermute | solution.py:27
  22.4 15.2 %collective-permute-start.2 = (bf16[16,1664]{1,0:T(8,128)(2,1)S(1)}, bf16[16,1664]{1,0:T(8,128)(2,1)S(1)}, u32[]{:S(2)}, u32[]{:S(2)}) collective-permute-start(bf16[16,1664]{1,0:T(8,128)(2,1)S(1)} %get-tuple-element.19), channel_id=1, source_target_pairs={{0,6},{2,8},{4,10},{6,12},{8,14},{10,0},{12,2},{14,4},{1,7},{3,9},... | collective-permute-start | bytes 159752 | tf_op jit(solution)/shard_map/ppermute | solution.py:27
  23.8 13.8 %collective-permute-start.3 = (bf16[16,1664]{1,0:T(8,128)(2,1)S(1)}, bf16[16,1664]{1,0:T(8,128)(2,1)S(1)}, u32[]{:S(2)}, u32[]{:S(2)}) collective-permute-start(bf16[16,1664]{1,0:T(8,128)(2,1)S(1)} %get-tuple-element.20), channel_id=1, source_target_pairs={{0,8},{2,10},{4,12},{6,14},{8,0},{10,2},{12,4},{14,6},{1,9},{3,11}... | collective-permute-start | bytes 159752 | tf_op jit(solution)/shard_map/ppermute | solution.py:27
  26.4 11.2 %collective-permute-start.4 = (bf16[16,1664]{1,0:T(8,128)(2,1)S(1)}, bf16[16,1664]{1,0:T(8,128)(2,1)S(1)}, u32[]{:S(2)}, u32[]{:S(2)}) collective-permute-start(bf16[16,1664]{1,0:T(8,128)(2,1)S(1)} %get-tuple-element.21), channel_id=1, source_target_pairs={{0,10},{2,12},{4,14},{6,0},{8,2},{10,4},{12,6},{14,8},{1,11},{3,13... | collective-permute-start | bytes 159752 | tf_op jit(solution)/shard_map/ppermute | solution.py:27
  28.6 9.0 %collective-permute-start.5 = (bf16[16,1664]{1,0:T(8,128)(2,1)S(1)}, bf16[16,1664]{1,0:T(8,128)(2,1)S(1)}, u32[]{:S(2)}, u32[]{:S(2)}) collective-permute-start(bf16[16,1664]{1,0:T(8,128)(2,1)S(1)} %get-tuple-element.22), channel_id=1, source_target_pairs={{0,12},{2,14},{4,0},{6,2},{8,4},{10,6},{12,8},{14,10},{1,13},{3,15... | collective-permute-start | bytes 159752 | tf_op jit(solution)/shard_map/ppermute | solution.py:27
  29.3 8.3 %collective-permute-start.6 = (bf16[16,1664]{1,0:T(8,128)(2,1)S(1)}, bf16[16,1664]{1,0:T(8,128)(2,1)S(1)}, u32[]{:S(2)}, u32[]{:S(2)}) collective-permute-start(bf16[16,1664]{1,0:T(8,128)(2,1)S(1)} %get-tuple-element.23), channel_id=1, source_target_pairs={{0,14},{2,0},{4,2},{6,4},{8,6},{10,8},{12,10},{14,12},{1,15},{3,1}... | collective-permute-start | bytes 159752 | tf_op jit(solution)/shard_map/ppermute | solution.py:27
  31.1 8.6 %copy-start.3 = (bf16[3072,8]{0,1:T(8,128)(2,1)S(1)}, bf16[3072,8]{0,1:T(8,128)(2,1)}, u32[]{:S(2)}) copy-start(bf16[3072,8]{0,1:T(8,128)(2,1)} %param.17) | copy-start | bytes 147460
  31.1 8.6 %copy-start.4 = (f32[3072]{0:T(1024)S(1)}, f32[3072]{0:T(1024)}, u32[]{:S(2)}) copy-start(f32[3072]{0:T(1024)} %param.16) | copy-start | bytes 36868
  37.9 1.8 %collective-permute-start.7 = (bf16[136,1536]{1,0:T(8,128)(2,1)S(1)}, bf16[136,1536]{1,0:T(8,128)(2,1)S(1)}, u32[]{:S(2)}, u32[]{:S(2)}) collective-permute-start(bf16[136,1536]{1,0:T(8,128)(2,1)S(1)} %get-tuple-element.25.refs_0_), channel_id=1, source_target_pairs={{0,1},{1,0},{2,3},{3,2},{4,5},{5,4},{6,7},{7,6},{8,9},{9,8},{10,11... | collective-permute-start | bytes 1253384 | tf_op jit(solution)/shard_map/ppermute | solution.py:22
